TPU v7x, 32 devices: a whole 2x2x4 slice. The times are simulated.
32 devices in a mesh: gz: 2 (over y), row: 4 (over z), col: 4 (over x, core).
Axes of the slice: x: 2, y: 2, z: 4, core: 2. Of those that a mesh axis runs over, the one named last changes fastest.
Arguments:
- lpanel: bfloat16 [2, 2, 1024, 2048], P(None, 'gz', 'row', 'col'), may hold values from -6 to 6
- upanel: bfloat16 [2, 2, 2048, 4096], P(None, 'gz', 'row', 'col'), may hold values from -0.125 to 0.125
- rowmap: int32 [2, 2, 4], P(None, 'gz', 'row'), may hold values from 0 to 1
- colmap: int32 [2, 2, 16], P(None, 'gz', 'col'), may hold values from 0 to 1
- blockmask: int32 [2, 2, 4, 16], P(None, 'gz', 'row', 'col'), may hold values 0 or 1
- front_blocks: bfloat16 [2, 2048, 2048], P(None, 'row', ('gz', 'col')), may hold values from -6 to 6
Outputs:
- front_update: bfloat16 [2, 2048, 2048], P(None, 'row', ('gz', 'col'))
All inputs are finite; a program needn't handle non-finite values. No bound on the sum of `blockmask` on one device may be relied on, other than what follows from the above.
Results may differ from a plain program's by a relative error of at most 0.008.
Values may be sent and summed in bfloat16 or wider, within the bound.
A program may use at most 64 MiB of HBM per device.

v0:
```python
import jax
import jax.numpy as jnp
from jax import lax
from jax.sharding import PartitionSpec as P

CB = 4
FRB = 2
LEVELS = 2


def column_sums(schur, cols_of, live, layers):
    width = schur.shape[0]
    blocks = schur.reshape(width, CB, width)
    targets = cols_of[:, None] == jnp.arange(layers, dtype=jnp.int32)[None, :]
    col_select = targets.astype(jnp.float32) * live.astype(jnp.float32)[:, None]
    return jnp.einsum("bjk,jl->lbk", blocks, col_select, precision=lax.Precision.HIGHEST)


def on_device(lpanel, upanel, rowmap, colmap, blockmask, front_blocks):
    layers = lax.axis_size("gz")
    width = lpanel.shape[2]
    tiles = []
    for depth in range(LEVELS):
        left_rows = lax.all_gather(lpanel[depth, 0], "col", axis=1, tiled=True)
        tiles.append(
            jnp.dot(
                left_rows,
                lax.all_gather(upanel[depth, 0], "row", axis=0, tiled=True),
                preferred_element_type=jnp.float32,
            )
        )
    results = []
    every_row = lax.all_gather(rowmap[:, :, 0], "gz", axis=1, tiled=True)
    for depth in range(LEVELS):
        sums = column_sums(tiles[depth], colmap[depth, 0], blockmask[depth, 0, 0], layers).astype(
            jnp.bfloat16
        )
        arrived = lax.all_to_all(sums, "gz", split_axis=0, concat_axis=0, tiled=True)
        row_select = (
            every_row[depth][:, None] == jnp.arange(FRB, dtype=jnp.int32)[None, :]
        ).astype(jnp.float32)
        placed = jnp.einsum(
            "sf,sbk->fbk", row_select, arrived.astype(jnp.float32), precision=lax.Precision.HIGHEST
        )
        placed = placed.reshape(FRB * width, width)
        results.append((front_blocks[depth].astype(jnp.float32) - placed).astype(jnp.bfloat16))
    return jnp.stack(results)


def solution(mesh):
    return jax.shard_map(
        on_device,
        mesh=mesh,
        in_specs=(
            P(None, "gz", "row", "col"),
            P(None, "gz", "row", "col"),
            P(None, "gz", "row"),
            P(None, "gz", "col"),
            P(None, "gz", "row", "col"),
            P(None, "row", ("gz", "col")),
        ),
        out_specs=P(None, "row", ("gz", "col")),
        check_vma=False,
    )
```

profile of v0, /device:TPU:0, one launch (start us, length us, event | category | flops | bytes accessed | tf_op | source)
XLA Modules:
  0.0 233.3 jit_solution(8685987046296502088)
XLA Ops:
  6.5 0.0 copy-start.4
  6.5 0.0 copy-start.1
  6.5 0.0 copy-start.2
  6.5 0.0 all-gather.14.cloned.1.call-start
  6.5 1.9 fusion.31
  8.5 0.0 all-gather.14.cloned.1.call-update
  8.5 0.0 all-gather.16.cloned.1.call-start
  8.5 3.0 %fusion.30 = (bf16[1,1,512,1024]{3,2,1,0:T(8,128)(2,1)}, bf16[1,1,512,1024]{3,2,1,0:T(8,128)(2,1)}) fusion(bf16[2,1,512,1024]{3,2,1,0:T(8,128)(2,1)} %param.7), kind=kLoop, calls=%fused_computation.43 | loop fusion | bytes 4194304 | tf_op jit(solution)/shard_map/slice | solution.py:28
  11.6 0.0 all-gather.16.cloned.1.call-update
  11.6 0.0 all-gather.10.cloned.1.call-start
  11.7 0.7 all-gather.10.cloned.1.call-update
  12.3 0.0 all-gather.12.cloned.1.call-start
  12.4 0.5 all-gather.12.cloned.1.call-update
  12.9 0.0 copy-done.4
  12.9 5.2 %all-gather = s32[2,2,1]{0,2,1:T(1,128)S(1)} all-gather(s32[2,1,1]{0,2,1:T(1,128)S(1)} %copy-done.4), channel_id=2, replica_groups=mesh['gz'=2,'row'=4,'col'=4] {'gz'}, dimensions={1}, use_global_device_ids=true | all-gather | bytes 24 | tf_op jit(solution)/shard_map/all_gather | solution.py:33
  18.1 0.2 slice_reduce_fusion.1
  18.4 0.0 copy-done.1
  18.4 0.0 copy-done.2
  18.4 10.0 %all-gather.14.cloned.1.call-done = bf16[1,1,256,2048]{3,2,1,0:T(8,128)(2,1)} async-done(((bf16[1,1,256,512]{3,2,1,0:T(8,128)(2,1)}), bf16[1,1,256,2048]{3,2,1,0:T(8,128)(2,1)}) %all-gather.14.cloned.1.call-update) | async-done | bytes 1048592 | tf_op jit(solution)/shard_map/all_gather | solution.py:24
  28.4 82.3 %all-gather.16.cloned.1.call-done = bf16[1,1,2048,1024]{3,2,1,0:T(8,128)(2,1)} async-done(((bf16[1,1,512,1024]{3,2,1,0:T(8,128)(2,1)}), bf16[1,1,2048,1024]{3,2,1,0:T(8,128)(2,1)}) %all-gather.16.cloned.1.call-update) | async-done | bytes 4194320 | tf_op jit(solution)/shard_map/all_gather | solution.py:28
  110.7 3.8 %fusion = f32[256,1024]{1,0:T(8,128)S(1)} fusion(bf16[1,1,2048,1024]{3,2,1,0:T(8,128)(2,1)} %all-gather.16.cloned.1.call-done, bf16[1,1,256,2048]{3,2,1,0:T(8,128)(2,1)} %all-gather.14.cloned.1.call-done), kind=kOutput, calls=%fused_computation | convolution fusion | flops 1073741824 | bytes 6291456 | tf_op jit(solution)/shard_map/dot_general | solution.py:26
  114.5 0.5 reshape.32
  115.0 1.9 convolution_convert_fusion
  116.8 0.8 copy.12
  117.6 3.4 %all-to-all-start.1 = ((bf16[2,256,256]{2,1,0:T(8,128)(2,1)}), bf16[2,256,256]{2,1,0:T(8,128)(2,1)S(1)}, u32[]{:S(2)}, u32[]{:S(2)}) async-start(bf16[2,256,256]{2,1,0:T(8,128)(2,1)} %copy.12), calls=%async_computation.1 | async-start | bytes 524288 | tf_op jit(solution)/shard_map/all_to_all | solution.py:38
  121.0 6.4 %all-gather.10.cloned.1.call-done = bf16[1,1,256,2048]{3,2,1,0:T(8,128)(2,1)} async-done(((bf16[1,1,256,512]{3,2,1,0:T(8,128)(2,1)}), bf16[1,1,256,2048]{3,2,1,0:T(8,128)(2,1)}) %all-gather.10.cloned.1.call-update) | async-done | bytes 1048592 | tf_op jit(solution)/shard_map/all_gather | solution.py:24
  127.5 82.2 %all-gather.12.cloned.1.call-done = bf16[1,1,2048,1024]{3,2,1,0:T(8,128)(2,1)} async-done(((bf16[1,1,512,1024]{3,2,1,0:T(8,128)(2,1)}), bf16[1,1,2048,1024]{3,2,1,0:T(8,128)(2,1)}) %all-gather.12.cloned.1.call-update) | async-done | bytes 4194320 | tf_op jit(solution)/shard_map/all_gather | solution.py:28
  209.7 3.8 %fusion.2 = f32[256,1024]{1,0:T(8,128)S(1)} fusion(bf16[1,1,2048,1024]{3,2,1,0:T(8,128)(2,1)} %all-gather.12.cloned.1.call-done, bf16[1,1,256,2048]{3,2,1,0:T(8,128)(2,1)} %all-gather.10.cloned.1.call-done), kind=kOutput, calls=%fused_computation.2 | convolution fusion | flops 1073741824 | bytes 6291456 | tf_op jit(solution)/shard_map/dot_general | solution.py:26
  213.4 0.0 copy-start
  213.5 0.5 reshape.30
  214.0 1.9 convolution_convert_fusion.1
  215.8 0.7 copy.9
  216.6 0.0 all-to-all-done.1
  216.6 3.4 %all-to-all-start = ((bf16[2,256,256]{2,1,0:T(8,128)(2,1)}), bf16[2,256,256]{2,1,0:T(8,128)(2,1)S(1)}, u32[]{:S(2)}, u32[]{:S(2)}) async-start(bf16[2,256,256]{2,1,0:T(8,128)(2,1)} %copy.9), calls=%async_computation | async-start | bytes 524288 | tf_op jit(solution)/shard_map/all_to_all | solution.py:38
  220.0 0.4 fusion.8
  220.5 4.8 %all-to-all-done = bf16[2,256,256]{2,1,0:T(8,128)(2,1)S(1)} async-done(((bf16[2,256,256]{2,1,0:T(8,128)(2,1)}), bf16[2,256,256]{2,1,0:T(8,128)(2,1)S(1)}, u32[]{:S(2)}, u32[]{:S(2)}) %all-to-all-start) | async-done | bytes 262176 | tf_op jit(solution)/shard_map/all_to_all | solution.py:38
  225.3 0.4 fusion.10
  225.8 0.0 copy-done
  225.8 0.2 fusion.7
  225.9 0.0 copy-start.3
  226.0 0.8 copy-done.3
  (5 shorter events, 0.1 us)
Async XLA Ops:
  6.5 6.4 %copy-start.4 = (s32[2,1,1]{0,2,1:T(1,128)S(1)}, s32[2,1,1]{0,2,1:T(1,128)}, u32[]{:S(2)}) copy-start(s32[2,1,1]{0,2,1:T(1,128)} %param.8) | copy-start | bytes 28
  6.5 11.8 %copy-start.1 = (s32[2,1,4]{2,1,0:T(1,128)S(1)}, s32[2,1,4]{2,1,0:T(1,128)}, u32[]{:S(2)}) copy-start(s32[2,1,4]{2,1,0:T(1,128)} %param.9) | copy-start | bytes 100
  6.5 11.8 %copy-start.2 = (s32[2,1,1,4]{3,2,1,0:T(1,128)S(1)}, s32[2,1,1,4]{3,2,1,0:T(1,128)}, u32[]{:S(2)}) copy-start(s32[2,1,1,4]{3,2,1,0:T(1,128)} %param.10) | copy-start | bytes 100
  6.5 21.8 %all-gather.14.cloned.1.call-start = ((), (), s32[]{:S(2)}) async-start(), calls=%async_computation.4 | async-start | bytes 1310720 | tf_op jit(solution)/shard_map/all_gather | solution.py:24
  8.5 102.2 %all-gather.16.cloned.1.call-start = ((), (), s32[]{:S(2)}) async-start(), calls=%async_computation.5 | async-start | bytes 5242880 | tf_op jit(solution)/shard_map/all_gather | solution.py:28
  11.6 115.9 %all-gather.10.cloned.1.call-start = ((), (), s32[]{:S(2)}) async-start(), calls=%async_computation.2 | async-start | bytes 1310720 | tf_op jit(solution)/shard_map/all_gather | solution.py:24
  12.3 197.3 %all-gather.12.cloned.1.call-start = ((), (), s32[]{:S(2)}) async-start(), calls=%async_computation.3 | async-start | bytes 5242880 | tf_op jit(solution)/shard_map/all_gather | solution.py:28
  117.6 99.0 %all-to-all-start.1 = ((bf16[2,256,256]{2,1,0:T(8,128)(2,1)}), bf16[2,256,256]{2,1,0:T(8,128)(2,1)S(1)}, u32[]{:S(2)}, u32[]{:S(2)}) async-start(bf16[2,256,256]{2,1,0:T(8,128)(2,1)} %copy.12), calls=%async_computation.1 | async-start | bytes 524288 | tf_op jit(solution)/shard_map/all_to_all | solution.py:38
  213.4 12.3 %copy-start = (bf16[2,512,256]{2,1,0:T(8,128)(2,1)S(1)}, bf16[2,512,256]{2,1,0:T(8,128)(2,1)}, u32[]{:S(2)}) copy-start(bf16[2,512,256]{2,1,0:T(8,128)(2,1)} %param.11) | copy-start | bytes 1572868
  216.6 8.7 %all-to-all-start = ((bf16[2,256,256]{2,1,0:T(8,128)(2,1)}), bf16[2,256,256]{2,1,0:T(8,128)(2,1)S(1)}, u32[]{:S(2)}, u32[]{:S(2)}) async-start(bf16[2,256,256]{2,1,0:T(8,128)(2,1)} %copy.9), calls=%async_computation | async-start | bytes 524288 | tf_op jit(solution)/shard_map/all_to_all | solution.py:38
  225.9 0.8 copy-start.3
Sparse Core Ops, SparseCore 0:
  8.9 19.4 all-gather.13
  29.9 80.7 all-gather.15
  112.3 15.1 all-gather.9
  128.9 80.7 all-gather.11
where the time goes:
time: 234 us; the launch traced here: 233 us
  waiting for transfers between devices  187 us (80%)
  between operations  13.3 us (6%)
  matrix products  12.1 us (5%)
  local copies, waits for them, and re-layouts  8.54 us (4%)
  starting transfers between devices  7.01 us (3%)
  blocking collectives  5.19 us (2%)
    all_gather x2, waiting for transfers between devices, on_device(): lax.all_gather(upanel[depth, 0], 'row', axis=0, tiled=True)  165 us
    all_gather x2, waiting for transfers between devices, on_device(): left_rows = lax.all_gather(lpanel[depth, 0], 'col', axis=1, tiled=True)  16.4 us
    dot_general x2, matrix products, on_device(): jnp.dot(left_rows, lax.all_gather(upanel[depth, 0], 'row', axis=0, tiled=...  7.52 us
    all_to_all x2, starting transfers between devices, on_device(): lax.all_to_all(sums, 'gz', split_axis=0, concat_axis=0, tiled=True)  6.89 us
    all_gather x1, blocking collectives, on_device(): every_row = lax.all_gather(rowmap[:, :, 0], 'gz', axis=1, tiled=True)  5.19 us
    all_to_all x2, waiting for transfers between devices, on_device(): lax.all_to_all(sums, 'gz', split_axis=0, concat_axis=0, tiled=True)  4.82 us
  transfers between devices with their start and end apart: 6, of which 5 were waited for; matrix products, arithmetic and copies ran while one was open for 7% of the time, Pallas kernels for 0%

commit v1 on v0

--- a/solution.py
+++ b/solution.py
@@ -21,7 +21,7 @@
     width = lpanel.shape[2]
     tiles = []
     for depth in range(LEVELS):
-        left_rows = lax.all_gather(lpanel[depth, 0], "col", axis=1, tiled=True)
+        left_rows = jnp.concatenate(lax.all_gather(lpanel[depth, 0], "col"), axis=1)
         tiles.append(
             jnp.dot(
                 left_rows,

time: 234 us -> 240 us (1.026)
  local copies, waits for them, and re-layouts: 8.54 us -> 23.5 us
  waiting for transfers between devices: 187 us -> 177 us
    all_gather x2, waiting for transfers between devices: 165 us -> 145 us  [on_device(): lax.all_gather(upanel[depth, 0], 'row', axis=0, tiled=True)]
    dot_general x0 -> x2, local copies, waits for them, and re-layouts: none -> 13.1 us  [on_device(): jnp.dot(left_rows, lax.all_gather(upanel[depth, 0], 'row', axis=0, tiled=...]
    all_gather x2, waiting for transfers between devices: 16.4 us -> 26.8 us  [on_device(): left_rows = jnp.concatenate(lax.all_gather(lpanel[depth, 0], 'col'), axis=1)]
    all_gather x0 -> x2, local copies, waits for them, and re-layouts: none -> 2.95 us  [on_device(): left_rows = jnp.concatenate(lax.all_gather(lpanel[depth, 0], 'col'), axis=1)]
  transfers between devices with their start and end apart: 6 -> 6, of which waited for: 5 -> 5; matrix products, arithmetic and copies ran while one was open for 7% -> 14% of each run, Pallas kernels for 0% -> 0%
where the time goes in v1:
time: 240 us; the launch traced here: 239 us
  waiting for transfers between devices  177 us (74%)
  local copies, waits for them, and re-layouts  23.5 us (10%)
  between operations  13.3 us (6%)
  matrix products  12.9 us (5%)
  starting transfers between devices  7.01 us (3%)
  blocking collectives  5.19 us (2%)
    all_gather x2, waiting for transfers between devices, on_device(): lax.all_gather(upanel[depth, 0], 'row', axis=0, tiled=True)  145 us
    all_gather x2, waiting for transfers between devices, on_device(): left_rows = jnp.concatenate(lax.all_gather(lpanel[depth, 0], 'col'), axis=1)  26.8 us
    dot_general x2, local copies, waits for them, and re-layouts, on_device(): jnp.dot(left_rows, lax.all_gather(upanel[depth, 0], 'row', axis=0, tiled=...  13.1 us
    dot_general x2, matrix products, on_device(): jnp.dot(left_rows, lax.all_gather(upanel[depth, 0], 'row', axis=0, tiled=...  7.37 us
    all_to_all x2, starting transfers between devices, on_device(): lax.all_to_all(sums, 'gz', split_axis=0, concat_axis=0, tiled=True)  6.89 us
    all_gather x1, blocking collectives, on_device(): every_row = lax.all_gather(rowmap[:, :, 0], 'gz', axis=1, tiled=True)  5.19 us
    all_to_all x2, waiting for transfers between devices, on_device(): lax.all_to_all(sums, 'gz', split_axis=0, concat_axis=0, tiled=True)  4.82 us
  transfers between devices with their start and end apart: 6, of which 5 were waited for; matrix products, arithmetic and copies ran while one was open for 14% of the time, Pallas kernels for 0%

profile of v1, /device:TPU:0, one launch (start us, length us, event | category | flops | bytes accessed | tf_op | source)
XLA Modules:
  0.0 239.5 jit_solution(16202264814897344558)
XLA Ops:
  6.5 0.0 copy-start.4
  6.5 0.0 copy-start.1
  6.5 0.0 copy-start.2
  6.5 0.0 all-gather.14.cloned.1.call-start
  6.5 1.9 fusion.27
  8.4 0.0 all-gather.14.cloned.1.call-update
  8.4 0.0 all-gather.10.cloned.1.call-start
  8.5 0.7 all-gather.10.cloned.1.call-update
  9.2 0.0 all-gather.16.cloned.1.call-start
  9.2 3.1 %fusion.26 = (bf16[1,1,512,1024]{3,2,1,0:T(8,128)(2,1)}, bf16[1,1,512,1024]{3,2,1,0:T(8,128)(2,1)}) fusion(bf16[2,1,512,1024]{3,2,1,0:T(8,128)(2,1)} %param.7), kind=kLoop, calls=%fused_computation.39 | loop fusion | bytes 4194304 | tf_op jit(solution)/shard_map/slice | solution.py:28
  12.3 0.0 all-gather.16.cloned.1.call-update
  12.3 0.0 all-gather.12.cloned.1.call-start
  12.4 0.5 all-gather.12.cloned.1.call-update
  12.9 0.0 copy-done.4
  12.9 5.2 %all-gather = s32[2,2,1]{0,2,1:T(1,128)S(1)} all-gather(s32[2,1,1]{0,2,1:T(1,128)S(1)} %copy-done.4), channel_id=2, replica_groups=mesh['gz'=2,'row'=4,'col'=4] {'gz'}, dimensions={1}, use_global_device_ids=true | all-gather | bytes 24 | tf_op jit(solution)/shard_map/all_gather | solution.py:33
  18.1 0.2 slice_reduce_fusion.1
  18.4 0.0 copy-done.1
  18.4 0.0 copy-done.2
  18.4 10.0 %all-gather.14.cloned.1.call-done = bf16[4,1,256,512]{3,2,1,0:T(8,128)(2,1)} async-done(((bf16[1,1,256,512]{3,2,1,0:T(8,128)(2,1)}), bf16[4,1,256,512]{3,2,1,0:T(8,128)(2,1)}) %all-gather.14.cloned.1.call-update) | async-done | bytes 1048592 | tf_op jit(solution)/shard_map/all_gather | solution.py:24
  28.4 1.5 copy.18
  29.8 16.8 %all-gather.10.cloned.1.call-done = bf16[4,1,256,512]{3,2,1,0:T(8,128)(2,1)} async-done(((bf16[1,1,256,512]{3,2,1,0:T(8,128)(2,1)}), bf16[4,1,256,512]{3,2,1,0:T(8,128)(2,1)}) %all-gather.10.cloned.1.call-update) | async-done | bytes 1048592 | tf_op jit(solution)/shard_map/all_gather | solution.py:24
  46.6 1.5 copy.11
  48.1 80.9 %all-gather.16.cloned.1.call-done = bf16[1,1,2048,1024]{3,2,1,0:T(8,128)(2,1)} async-done(((bf16[1,1,512,1024]{3,2,1,0:T(8,128)(2,1)}), bf16[1,1,2048,1024]{3,2,1,0:T(8,128)(2,1)}) %all-gather.16.cloned.1.call-update) | async-done | bytes 4194320 | tf_op jit(solution)/shard_map/all_gather | solution.py:28
  129.0 6.5 %copy.19 = bf16[1024,2048]{1,0:T(8,128)(2,1)} copy(bf16[1024,2048]{0,1:T(8,128)(2,1)} %bitcast.56) | data formatting | bytes 8388608 | tf_op jit(solution)/shard_map/dot_general | solution.py:26
  135.5 3.9 %fusion.29 = f32[256,4,256]{2,0,1:T(8,128)S(1)} fusion(bf16[256,2048,1]{0,1,2:T(8,128)(2,1)S(1)} %bitcast.62, bf16[4,256,2048]{2,1,0:T(8,128)(2,1)} %bitcast.57), kind=kOutput, calls=%fused_computation.42 | convolution fusion | flops 1073741824 | bytes 6291456 | tf_op jit(solution)/shard_map/dot_general | solution.py:26
  139.4 2.3 convolution_convert_fusion
  141.7 0.7 copy.22
  142.5 3.4 %all-to-all-start.1 = ((bf16[2,256,256]{2,1,0:T(8,128)(2,1)}), bf16[2,256,256]{2,1,0:T(8,128)(2,1)S(1)}, u32[]{:S(2)}, u32[]{:S(2)}) async-start(bf16[2,256,256]{2,1,0:T(8,128)(2,1)} %copy.22), calls=%async_computation.1 | async-start | bytes 524288 | tf_op jit(solution)/shard_map/all_to_all | solution.py:38
  145.9 63.8 %all-gather.12.cloned.1.call-done = bf16[1,1,2048,1024]{3,2,1,0:T(8,128)(2,1)} async-done(((bf16[1,1,512,1024]{3,2,1,0:T(8,128)(2,1)}), bf16[1,1,2048,1024]{3,2,1,0:T(8,128)(2,1)}) %all-gather.12.cloned.1.call-update) | async-done | bytes 4194320 | tf_op jit(solution)/shard_map/all_gather | solution.py:28
  209.7 6.6 %copy.12 = bf16[1024,2048]{1,0:T(8,128)(2,1)} copy(bf16[1024,2048]{0,1:T(8,128)(2,1)} %bitcast.55) | data formatting | bytes 8388608 | tf_op jit(solution)/shard_map/dot_general | solution.py:26
  216.2 3.5 %fusion.28 = f32[256,4,256]{2,0,1:T(8,128)S(1)} fusion(bf16[256,2048,1]{0,1,2:T(8,128)(2,1)S(1)} %bitcast.61, bf16[4,256,2048]{2,1,0:T(8,128)(2,1)} %bitcast.58), kind=kOutput, calls=%fused_computation.41 | convolution fusion | flops 1073741824 | bytes 6291456 | tf_op jit(solution)/shard_map/dot_general | solution.py:26
  219.7 0.0 copy-start
  219.7 2.3 convolution_convert_fusion.1
  222.1 0.7 copy.15
  222.8 0.0 all-to-all-done.1
  222.8 3.4 %all-to-all-start = ((bf16[2,256,256]{2,1,0:T(8,128)(2,1)}), bf16[2,256,256]{2,1,0:T(8,128)(2,1)S(1)}, u32[]{:S(2)}, u32[]{:S(2)}) async-start(bf16[2,256,256]{2,1,0:T(8,128)(2,1)} %copy.15), calls=%async_computation | async-start | bytes 524288 | tf_op jit(solution)/shard_map/all_to_all | solution.py:38
  226.3 0.4 fusion.4
  226.7 4.8 %all-to-all-done = bf16[2,256,256]{2,1,0:T(8,128)(2,1)S(1)} async-done(((bf16[2,256,256]{2,1,0:T(8,128)(2,1)}), bf16[2,256,256]{2,1,0:T(8,128)(2,1)S(1)}, u32[]{:S(2)}, u32[]{:S(2)}) %all-to-all-start) | async-done | bytes 262176 | tf_op jit(solution)/shard_map/all_to_all | solution.py:38
  231.6 0.4 fusion.6
  232.0 0.0 copy-done
  232.0 0.1 fusion.3
  232.2 0.0 copy-start.3
  232.2 0.8 copy-done.3
  (5 shorter events, 0.1 us)
Async XLA Ops:
  6.5 6.4 %copy-start.4 = (s32[2,1,1]{0,2,1:T(1,128)S(1)}, s32[2,1,1]{0,2,1:T(1,128)}, u32[]{:S(2)}) copy-start(s32[2,1,1]{0,2,1:T(1,128)} %param.8) | copy-start | bytes 28
  6.5 11.8 %copy-start.1 = (s32[2,1,4]{2,1,0:T(1,128)S(1)}, s32[2,1,4]{2,1,0:T(1,128)}, u32[]{:S(2)}) copy-start(s32[2,1,4]{2,1,0:T(1,128)} %param.9) | copy-start | bytes 100
  6.5 11.8 %copy-start.2 = (s32[2,1,1,4]{3,2,1,0:T(1,128)S(1)}, s32[2,1,1,4]{3,2,1,0:T(1,128)}, u32[]{:S(2)}) copy-start(s32[2,1,1,4]{3,2,1,0:T(1,128)} %param.10) | copy-start | bytes 100
  6.5 21.8 %all-gather.14.cloned.1.call-start = ((), (), s32[]{:S(2)}) async-start(), calls=%async_computation.4 | async-start | bytes 1310720 | tf_op jit(solution)/shard_map/all_gather | solution.py:24
  8.4 38.2 %all-gather.10.cloned.1.call-start = ((), (), s32[]{:S(2)}) async-start(), calls=%async_computation.2 | async-start | bytes 1310720 | tf_op jit(solution)/shard_map/all_gather | solution.py:24
  9.2 119.8 %all-gather.16.cloned.1.call-start = ((), (), s32[]{:S(2)}) async-start(), calls=%async_computation.5 | async-start | bytes 5242880 | tf_op jit(solution)/shard_map/all_gather | solution.py:28
  12.3 197.3 %all-gather.12.cloned.1.call-start = ((), (), s32[]{:S(2)}) async-start(), calls=%async_computation.3 | async-start | bytes 5242880 | tf_op jit(solution)/shard_map/all_gather | solution.py:28
  142.5 80.4 %all-to-all-start.1 = ((bf16[2,256,256]{2,1,0:T(8,128)(2,1)}), bf16[2,256,256]{2,1,0:T(8,128)(2,1)S(1)}, u32[]{:S(2)}, u32[]{:S(2)}) async-start(bf16[2,256,256]{2,1,0:T(8,128)(2,1)} %copy.22), calls=%async_computation.1 | async-start | bytes 524288 | tf_op jit(solution)/shard_map/all_to_all | solution.py:38
  219.7 12.3 %copy-start = (bf16[2,512,256]{2,1,0:T(8,128)(2,1)S(1)}, bf16[2,512,256]{2,1,0:T(8,128)(2,1)}, u32[]{:S(2)}) copy-start(bf16[2,512,256]{2,1,0:T(8,128)(2,1)} %param.11) | copy-start | bytes 1572868
  222.8 8.7 %all-to-all-start = ((bf16[2,256,256]{2,1,0:T(8,128)(2,1)}), bf16[2,256,256]{2,1,0:T(8,128)(2,1)S(1)}, u32[]{:S(2)}, u32[]{:S(2)}) async-start(bf16[2,256,256]{2,1,0:T(8,128)(2,1)} %copy.15), calls=%async_computation | async-start | bytes 524288 | tf_op jit(solution)/shard_map/all_to_all | solution.py:38
  232.2 0.8 copy-start.3
Sparse Core Ops, SparseCore 0:
  8.9 19.4 all-gather.13
  29.9 16.6 all-gather.9
  48.2 80.7 all-gather.15
  130.4 79.2 all-gather.11
